TPU v7x, 32 devices: a whole 2x2x4 slice. The times are simulated.
32 devices in a mesh: row: 8 (over z, y), col: 4 (over x, core).
Axes of the slice: x: 2, y: 2, z: 4, core: 2. Of those that a mesh axis runs over, the one named last changes fastest.
Arguments:
- image_in: bfloat16 [2048, 1536], P('row', 'col'), may hold values from -6 to 6
- text_in: bfloat16 [2464, 1536], P('row', 'col'), may hold values from -6 to 6
- condition: bfloat16 [16, 1536], P(None, 'row'), may hold values from -6 to 6
- ranges: int32 [16, 2], P('row'), may hold values from 0 to 192, as said below
- mod_weight: bfloat16 [1, 1536, 2, 6, 1536], P(None, 'row', None, None, 'col'), may hold values from -0.15625 to 0.15625
- qkv_weight: bfloat16 [1, 1536, 2, 3, 1536], P(None, 'row', None, None, 'col'), may hold values from -0.15625 to 0.15625
- out_weight: bfloat16 [1, 1536, 2, 1536], P(None, 'row', None, 'col'), may hold values from -2.5 to 2.5
- up_weight: bfloat16 [1, 1536, 2, 6144], P(None, 'row', None, 'col'), may hold values from -0.15625 to 0.15625
- down_weight: bfloat16 [1, 1536, 2, 6144], P(None, 'row', None, 'col'), may hold values from -0.078125 to 0.078125
- image_cot: bfloat16 [2048, 1536], P('row', 'col'), may hold values from -6 to 6
- text_cot: bfloat16 [2464, 1536], P('row', 'col'), may hold values from -6 to 6
Outputs:
- image_out: float32 [2048, 1536], P('row', 'col')
- text_out: float32 [2464, 1536], P('row', 'col')
- grad_image: float32 [2048, 1536], P('row', 'col')
- grad_text: float32 [2464, 1536], P('row', 'col')
- grad_cond: float32 [16, 1536], P(None, 'row')
- grad_mod: float32 [1, 1536, 2, 6, 1536], P(None, 'row', None, None, 'col')
- grad_qkv: float32 [1, 1536, 2, 3, 1536], P(None, 'row', None, None, 'col')
- grad_out: float32 [1, 1536, 2, 1536], P(None, 'row', None, 'col')
- grad_up: float32 [1, 1536, 2, 6144], P(None, 'row', None, 'col')
- grad_down: float32 [1, 1536, 2, 6144], P(None, 'row', None, 'col')
Inputs may be any that keep to these rules, and one draw needn't show every extreme that they name: `ranges`: each index of row has 2 slots; the first always holds 154 text rows and a multiple of 64 image rows; the second is empty or holds 154 text rows and exactly the image rows the first leaves over, so that index's 256 image rows are full.
All inputs are finite; a program needn't handle non-finite values.
Results may differ from a plain program's by a relative error of at most 0.015.
The roundings to bfloat16 on the way count: a program that leaves them out, or rounds other values in their place, can miss the bound.
Values may be sent and summed in bfloat16 or wider, within the bound.
A program may use at most 320 MiB of HBM per device.

v0:
```python
import math
import jax
import jax.numpy as jnp
from jax import lax
from jax.sharding import PartitionSpec as P

D = 1536
LAYERS = 1
IMG_DEV = 256
HD = 64
TXT_DEV = 308
EPSILON = 1e-06
HIGHEST = lax.Precision.HIGHEST


def slot_table(lengths, image_rows, text_rows):
    ends = jnp.cumsum(lengths, axis=0, dtype=jnp.int32)
    starts = ends - lengths
    slot_ids = jnp.arange(lengths.shape[0], dtype=jnp.int32)
    tables = []
    segments = []
    for column, amount in ((0, image_rows), (1, text_rows)):
        places = jnp.arange(amount, dtype=jnp.int32)[:, None]
        inside = ((places >= starts[None, :, column]) & (places < ends[None, :, column])).astype(
            jnp.int32
        )
        tables.append(inside.astype(jnp.float32))
        filled = jnp.sum(inside, axis=1, dtype=jnp.int32)
        segments.append(
            jnp.sum(inside * slot_ids[None, :], axis=1, dtype=jnp.int32)
            + lengths.shape[0] * (1 - filled)
        )
    return (jnp.concatenate(tables, axis=0), jnp.concatenate(segments, axis=0))


def stream_dot(left, right_image, right_text):
    upper = jnp.dot(left[:IMG_DEV], right_image, preferred_element_type=jnp.float32)
    lower = jnp.dot(left[IMG_DEV:], right_text, preferred_element_type=jnp.float32)
    return jnp.concatenate([upper, lower], axis=0)


def stream_outer(left, right):
    upper = jnp.einsum(
        "nk,nf->kf", left[:IMG_DEV], right[:IMG_DEV], preferred_element_type=jnp.float32
    )
    lower = jnp.einsum(
        "nk,nf->kf", left[IMG_DEV:], right[IMG_DEV:], preferred_element_type=jnp.float32
    )
    return (upper, lower)


def row_mod(slot_ones, mod_mine, layer_index, component):
    upper = jnp.dot(slot_ones[:IMG_DEV], mod_mine[:, layer_index, 0, component], precision=HIGHEST)
    lower = jnp.dot(slot_ones[IMG_DEV:], mod_mine[:, layer_index, 1, component], precision=HIGHEST)
    return jnp.concatenate([upper, lower], axis=0)


def slot_sums(slot_ones, rows):
    upper = jnp.dot(slot_ones[:IMG_DEV].T, rows[:IMG_DEV], precision=HIGHEST)
    lower = jnp.dot(slot_ones[IMG_DEV:].T, rows[IMG_DEV:], precision=HIGHEST)
    return jnp.stack([upper, lower], axis=1)


def feature_sums(first, second):
    return lax.psum((jnp.sum(first, axis=1), jnp.sum(second, axis=1)), "col")


def normalize(hidden):
    totals, squares = feature_sums(hidden, hidden * hidden)
    center = totals / D
    spread = squares / D - center * center
    scaling = lax.rsqrt(spread + EPSILON)
    return ((hidden - center[:, None]) * scaling[:, None], scaling[:, None])


def norm_back(grad_hat, normed, scaling):
    first, second = feature_sums(grad_hat, grad_hat * normed)
    return scaling * (grad_hat - first[:, None] / D - normed * (second[:, None] / D))


def gelu_slope(value):
    coeff = math.sqrt(2.0 / math.pi)
    tangent = jnp.tanh(coeff * (value + 0.044715 * value * value * value))
    return 0.5 * (1.0 + tangent) + 0.5 * value * (1.0 - tangent * tangent) * coeff * (
        1.0 + 3.0 * 0.044715 * value * value
    )


def silu_slope(value):
    sigma = jax.nn.sigmoid(value)
    return sigma * (1.0 + value * (1.0 - sigma))


def gather_features(values):
    return lax.all_gather(values, "col", axis=1, tiled=True)


def gather_grads(values):
    return lax.all_gather(values, "col", axis=1, tiled=True)


def scatter_features(values):
    return lax.psum_scatter(values, "col", scatter_dimension=1, tiled=True)


def scatter_back(values):
    return lax.psum_scatter(values, "col", scatter_dimension=1, tiled=True)


def spread_grads(terms, row_count):
    return lax.psum_scatter(
        terms(jnp.int32(0), row_count * lax.axis_size("row")),
        "row",
        scatter_dimension=0,
        tiled=True,
    )


def fold_rows(left, weight):
    portion = lax.all_gather(weight, "row", axis=0, tiled=True)
    return stream_dot(left, portion[:, 0], portion[:, 1])


def map_rows(left, weight):
    portion = lax.all_gather(weight, "row", axis=0, tiled=True)
    return stream_dot(left, portion[:, 0].T, portion[:, 1].T)


def apply_in(left, weight):
    result = fold_rows(left, weight)
    return result


def apply_out(left, weight):
    result = map_rows(left, weight)
    return result


def mlp_part(operands):
    grad_full, gathered, grad_lifted, activated = operands
    up_image, up_text = stream_outer(gathered, grad_lifted)
    down_image, down_text = stream_outer(grad_full, activated)
    image_part = jnp.concatenate([up_image, down_image], axis=1)
    text_part = jnp.concatenate([up_text, down_text], axis=1)
    return jnp.stack([image_part, text_part], axis=1)


def attention_part(operands):
    grad_full, gathered, grad_projected, mixed = operands
    qkv_image, qkv_text = stream_outer(gathered, grad_projected)
    out_image, out_text = stream_outer(grad_full, mixed)
    image_part = jnp.concatenate([qkv_image, out_image], axis=1)
    text_part = jnp.concatenate([qkv_text, out_text], axis=1)
    return jnp.stack([image_part, text_part], axis=1)


def attend_head(operands, segments, scale):
    queries, key_rows, value_rows = operands
    scores = jnp.dot(queries, key_rows.T, preferred_element_type=jnp.float32) * scale
    allowed = segments[:, None] == segments[None, :]
    scores = jnp.where(allowed, scores, -jnp.inf)
    highest = jnp.max(scores, axis=1, keepdims=True)
    log_total = highest + jnp.log(jnp.sum(jnp.exp(scores - highest), axis=1, keepdims=True))
    weights = jnp.exp(scores - log_total).astype(jnp.bfloat16)
    output = jnp.dot(weights, value_rows, preferred_element_type=jnp.float32).astype(jnp.bfloat16)
    return (output, log_total[:, 0])


def attend_back_head(operands, segments, scale):
    queries, key_rows, value_rows, output, grad_output, log_total = operands
    scores = jnp.dot(queries, key_rows.T, preferred_element_type=jnp.float32) * scale
    allowed = segments[:, None] == segments[None, :]
    scores = jnp.where(allowed, scores, -jnp.inf)
    probs = jnp.exp(scores - log_total[:, None])
    grad_values = jnp.dot(
        probs.astype(jnp.bfloat16).T, grad_output, preferred_element_type=jnp.float32
    )
    grad_probs = jnp.dot(grad_output, value_rows.T, preferred_element_type=jnp.float32)
    inner = jnp.sum(
        grad_output.astype(jnp.float32) * output.astype(jnp.float32), axis=1, keepdims=True
    )
    grad_scores = (probs * (grad_probs - inner) * scale).astype(jnp.bfloat16)
    grad_queries = jnp.dot(grad_scores, key_rows, preferred_element_type=jnp.float32)
    grad_keys = jnp.dot(grad_scores.T, queries, preferred_element_type=jnp.float32)
    return jnp.stack([grad_queries, grad_keys, grad_values], axis=0).astype(jnp.bfloat16)


def per_device(
    image_in,
    text_in,
    condition,
    ranges,
    mod_weight,
    qkv_weight,
    out_weight,
    up_weight,
    down_weight,
    image_cot,
    text_cot,
):
    slot_ones, segments = slot_table(ranges, IMG_DEV, TXT_DEV)
    col_width = image_in.shape[1]
    ff_width = up_weight.shape[3]
    row_count = qkv_weight.shape[1]
    heads_here = col_width // HD
    scale = 1.0 / math.sqrt(HD)
    silu_cond = jax.nn.silu(condition.astype(jnp.float32)).astype(jnp.bfloat16)
    mod_terms = jnp.einsum(
        "sd,ldxkf->slxkf", silu_cond, mod_weight, preferred_element_type=jnp.float32
    )
    mod_mine = lax.psum_scatter(mod_terms, "row", scatter_dimension=0, tiled=True)
    hidden = jnp.concatenate([image_in, text_in], axis=0).astype(jnp.float32)
    layer_index = 0
    qkv_local = qkv_weight[layer_index].reshape(row_count, 2, 3 * col_width)
    whole = (None, None, None, None)
    mods = [row_mod(slot_ones, mod_mine, layer_index, part_no) for part_no in range(6)]
    normed_one, scaling_one = normalize(hidden)
    modulated_one = (normed_one * (1.0 + mods[1]) + mods[0]).astype(jnp.bfloat16)
    gathered_one = gather_features(modulated_one)
    projected = apply_in(gathered_one, qkv_local).astype(jnp.bfloat16)
    heads_form = projected.reshape(-1, 3, heads_here, HD).transpose(1, 2, 0, 3)
    attended, log_totals = lax.map(
        lambda operands: attend_head(operands, segments, scale),
        (heads_form[0], heads_form[1], heads_form[2]),
    )
    mixed = attended.transpose(1, 0, 2).reshape(-1, col_width)
    branch_one = scatter_features(apply_out(mixed, out_weight[layer_index]))
    midway = hidden + mods[2] * branch_one
    normed_two, scaling_two = normalize(midway)
    modulated_two = (normed_two * (1.0 + mods[4]) + mods[3]).astype(jnp.bfloat16)
    gathered_two = gather_features(modulated_two)
    lifted = apply_in(gathered_two, up_weight[layer_index])
    activated = jax.nn.gelu(lifted, approximate=True).astype(jnp.bfloat16)
    branch_two = scatter_features(apply_out(activated, down_weight[layer_index]))
    hidden = midway + mods[5] * branch_two
    saved = [
        (
            whole,
            normed_one,
            scaling_one,
            gathered_one,
            heads_form,
            attended,
            log_totals,
            mixed,
            branch_one,
            normed_two,
            scaling_two,
            gathered_two,
            lifted,
            activated,
            branch_two,
        )
    ]
    image_out = hidden[:IMG_DEV]
    text_out = hidden[IMG_DEV:]
    grad_hidden = jnp.concatenate([image_cot, text_cot], axis=0).astype(jnp.float32)
    grads_qkv = [None] * LAYERS
    grads_out = [None] * LAYERS
    grads_up = [None] * LAYERS
    grads_down = [None] * LAYERS
    grads_slots = [None] * LAYERS
    for layer_index in reversed(range(LAYERS)):
        (
            whole,
            normed_one,
            scaling_one,
            gathered_one,
            heads_form,
            attended,
            log_totals,
            mixed,
            branch_one,
            normed_two,
            scaling_two,
            gathered_two,
            lifted,
            activated,
            branch_two,
        ) = saved[layer_index]
        qkv_local = qkv_weight[layer_index].reshape(row_count, 2, 3 * col_width)
        mods = [row_mod(slot_ones, mod_mine, layer_index, part_no) for part_no in range(6)]
        grad_branch_two = (grad_hidden * mods[5]).astype(jnp.bfloat16)
        gate_two_rows = grad_hidden * branch_two
        grad_full_two = gather_grads(grad_branch_two)
        grad_act = apply_in(grad_full_two, down_weight[layer_index])
        grad_lifted = (grad_act * gelu_slope(lifted)).astype(jnp.bfloat16)
        mlp_operands = (grad_full_two, gathered_two, grad_lifted, activated)
        mlp_grads = spread_grads(lambda offset, amount: mlp_part(mlp_operands), row_count)
        grads_up[layer_index] = mlp_grads[:, :, :ff_width]
        grads_down[layer_index] = mlp_grads[:, :, ff_width:]
        grad_mod_two = scatter_back(apply_out(grad_lifted, up_weight[layer_index]))
        scale_two_rows = grad_mod_two * normed_two
        grad_hidden = grad_hidden + norm_back(
            grad_mod_two * (1.0 + mods[4]), normed_two, scaling_two
        )
        grad_branch_one = (grad_hidden * mods[2]).astype(jnp.bfloat16)
        gate_one_rows = grad_hidden * branch_one
        grad_full_one = gather_grads(grad_branch_one)
        grad_mixed = apply_in(grad_full_one, out_weight[layer_index]).astype(jnp.bfloat16)
        grad_heads = grad_mixed.reshape(-1, heads_here, HD).transpose(1, 0, 2)
        grad_parts = lax.map(
            lambda operands: attend_back_head(operands, segments, scale),
            (heads_form[0], heads_form[1], heads_form[2], attended, grad_heads, log_totals),
        )
        grad_projected = grad_parts.transpose(2, 1, 0, 3).reshape(-1, 3 * col_width)
        attention_operands = (grad_full_one, gathered_one, grad_projected, mixed)
        attention_grads = spread_grads(
            lambda offset, amount: attention_part(attention_operands), row_count
        )
        grads_qkv[layer_index] = attention_grads[:, :, : 3 * col_width].reshape(
            row_count, 2, 3, col_width
        )
        grads_out[layer_index] = attention_grads[:, :, 3 * col_width :]
        grad_mod_one = scatter_back(apply_out(grad_projected, qkv_local))
        scale_one_rows = grad_mod_one * normed_one
        grad_hidden = grad_hidden + norm_back(
            grad_mod_one * (1.0 + mods[1]), normed_one, scaling_one
        )
        rows_list = [
            grad_mod_one,
            scale_one_rows,
            gate_one_rows,
            grad_mod_two,
            scale_two_rows,
            gate_two_rows,
        ]
        grads_slots[layer_index] = jnp.stack(
            [slot_sums(slot_ones, rows) for rows in rows_list], axis=2
        )
    mod_all = lax.all_gather(jnp.stack(grads_slots, axis=1), "row", axis=0, tiled=True)
    grad_mod = jnp.einsum(
        "sd,slxkf->ldxkf", silu_cond.astype(jnp.float32), mod_all, precision=HIGHEST
    )
    cond_part = jnp.einsum(
        "slxkf,ldxkf->sd", mod_all, mod_weight.astype(jnp.float32), precision=HIGHEST
    )
    cond_total = lax.psum(cond_part, "col")
    grad_cond = cond_total * silu_slope(condition.astype(jnp.float32))
    grad_image = grad_hidden[:IMG_DEV]
    grad_text = grad_hidden[IMG_DEV:]
    return (
        image_out,
        text_out,
        grad_image,
        grad_text,
        grad_cond,
        grad_mod,
        jnp.stack(grads_qkv),
        jnp.stack(grads_out),
        jnp.stack(grads_up),
        jnp.stack(grads_down),
    )


def solution(mesh):
    return jax.shard_map(
        per_device,
        mesh=mesh,
        in_specs=(
            P("row", "col"),
            P("row", "col"),
            P(None, "row"),
            P("row", None),
            P(None, "row", None, None, "col"),
            P(None, "row", None, None, "col"),
            P(None, "row", None, "col"),
            P(None, "row", None, "col"),
            P(None, "row", None, "col"),
            P("row", "col"),
            P("row", "col"),
        ),
        out_specs=(
            P("row", "col"),
            P("row", "col"),
            P("row", "col"),
            P("row", "col"),
            P(None, "row"),
            P(None, "row", None, None, "col"),
            P(None, "row", None, None, "col"),
            P(None, "row", None, "col"),
            P(None, "row", None, "col"),
            P(None, "row", None, "col"),
        ),
        check_vma=False,
    )
```

profile of v0, /device:TPU:0, one launch (start us, length us, event | category | flops | bytes accessed | tf_op | source)
XLA Modules:
  0.0 2627.9 jit_solution(4866509215842069157)
XLA Ops:
  15.9 8.5 all-reduce.6
  24.7 61.2 %all-reduce.11.cloned.1.call-done = f32[16,1,2,6,384]{4,0,3,2,1:T(8,128)} async-done(((f32[16,1,2,6,384]{4,0,3,2,1:T(8,128)}), f32[16,1,2,6,384]{4,0,3,2,1:T(8,128)}) %all-reduce.11.cloned.1.call-update) | async-done | bytes 294928
  95.3 100.8 %all-gather.15.cloned.1.call-done = bf16[1536,2,1152]{2,0,1:T(8,128)(2,1)} async-done(((bf16[192,2,1152]{2,0,1:T(8,128)(2,1)}), bf16[1536,2,1152]{2,0,1:T(8,128)(2,1)}) %all-gather.15.cloned.1.call-update) | async-done | bytes 7077904 | tf_op jit(solution)/shard_map/all_gather | solution.py:120
  196.0 6.6 slice_bitcast_fusion.13
  202.6 5.8 copy.120
  208.4 5.8 copy.119
  214.2 2.8 all-gather.13.cloned.1.call-done
  217.0 4.5 convolution_convert_fusion.4
  221.4 2.3 convolution_convert_fusion.5
  229.1 16.3 while.22
  249.0 22.4 all-gather.23.cloned.1.call-done
  271.4 2.2 fusion.73
  282.7 2.7 copy.125
  291.0 2.3 fusion.162
  294.8 2.3 fusion.167
  297.1 17.9 reduce-scatter.6.cloned.1.call-done
  316.8 5.9 all-reduce.5
  322.7 2.2 fusion.100
  325.0 12.6 all-gather.19.cloned.1.call-done
  337.6 140.0 %all-gather.27.cloned.1.call-done = bf16[1,1536,2,1536]{3,1,2,0:T(8,128)(2,1)} async-done(((bf16[1,192,2,1536]{3,1,2,0:T(8,128)(2,1)}), bf16[1,1536,2,1536]{3,1,2,0:T(8,128)(2,1)}) %all-gather.27.cloned.1.call-update) | async-done | bytes 9437200 | tf_op jit(solution)/shard_map/all_gather | solution.py:125
  477.7 5.2 fusion.44
  482.9 5.3 fusion.46
  488.2 127.7 %all-gather.25.cloned.1.call-done = bf16[1,1536,2,1536]{3,1,2,0:T(8,128)(2,1)} async-done(((bf16[1,192,2,1536]{3,1,2,0:T(8,128)(2,1)}), bf16[1,1536,2,1536]{3,1,2,0:T(8,128)(2,1)}) %all-gather.25.cloned.1.call-update) | async-done | bytes 9437200 | tf_op jit(solution)/shard_map/all_gather | solution.py:120
  615.9 20.9 all-gather.17.cloned.1.call-done
  636.8 4.4 fusion.43
  642.2 2.7 fusion.41
  644.8 4.1 fusion.66
  654.3 4.1 fusion.45
  658.4 4.6 fusion.47
  665.1 29.2 %reduce-scatter.10.cloned.1.call-done = f32[564,384]{1,0:T(8,128)} async-done(((f32[564,1536]{1,0:T(8,128)}), f32[564,384]{1,0:T(8,128)}) %reduce-scatter.10.cloned.1.call-update) | async-done | bytes 866320 | tf_op jit(solution)/shard_map/reduce_scatter | solution.py:107
  696.2 6.4 all-reduce.4
  703.3 34.0 %reduce-scatter.8.cloned.1.call-done = f32[564,384]{1,0:T(8,128)} async-done(((f32[564,1536]{1,0:T(8,128)}), f32[564,384]{1,0:T(8,128)}) %reduce-scatter.8.cloned.1.call-update) | async-done | bytes 866320 | tf_op jit(solution)/shard_map/reduce_scatter | solution.py:103
  737.4 4.4 convert_multiply_fusion.2
  743.6 9.1 reduce-scatter.12.cloned.1.call-start
  752.7 2.9 slice_bitcast_fusion.15
  755.6 2.4 copy.128
  759.4 4.9 all-gather.21.cloned.1.call-done
  764.3 2.4 convolution_convert_fusion.6
  769.1 64.8 %while.23 = (s32[]{:T(128)}, bf16[6,3,564,64]{2,3,0,1:T(8,128)(2,1)}, s32[564]{0:T(1024)}, bf16[6,564,64]{2,1,0:T(8,128)(2,1)}, bf16[6,564,64]{2,1,0:T(8,128)(2,...) while((s32[]{:T(128)}, ...), condition=%wide.region_27.28_spmd, body=%wide.region_25.27_spmd.sunk | while | flops 207346144 | bytes 8018613 | solution.py:302
  836.3 4.0 fusion.48
  840.3 3.2 fusion.50
  847.6 2.2 fusion.101
  849.8 4.4 fusion.132
  854.1 4.9 fusion.114
  859.0 8.2 maximum_bitcast_fusion.4
  867.3 7.8 maximum_bitcast_fusion.3
  875.0 14.7 pad_maximum_fusion.1
  889.7 28.5 %copy.139 = f32[1536,2,1536]{2,1,0:T(2,128)} copy(f32[1536,2,1536]{0,2,1:T(8,128)} %pad_maximum_fusion.1) | data formatting | bytes 37748736 | tf_op jit(solution)/shard_map/stack | solution.py:154
  918.5 3.0 fusion.125
  921.5 5.6 fusion.122
  927.2 5.1 fusion.107
  932.2 5.1 fusion.104
  937.3 7.8 maximum_bitcast_fusion.2
  945.1 11.3 maximum_bitcast_fusion.1
  956.4 21.2 pad_maximum_fusion
  977.5 55.5 %copy.141 = f32[1536,2,3072]{2,1,0:T(2,128)} copy(f32[1536,2,3072]{0,2,1:T(8,128)} %pad_maximum_fusion) | data formatting | bytes 75497472 | tf_op jit(solution)/shard_map/stack | solution.py:145
  1054.0 33.8 %all-gather.3 = f32[16,2,6,384]{3,1,2,0:T(2,128)S(1)} all-gather(f32[2,2,6,384]{3,1,2,0:T(2,128)S(1)} %copy.135), channel_id=5, replica_groups=mesh['row'=8,'col'=4] {'row'}, dimensions={0}, use_global_device_ids=true | all-gather | bytes 331776 | tf_op jit(solution)/shard_map/all_gather | solution.py:331
  1090.0 11.9 all-reduce.3
  1107.0 4.5 copy.142
  1112.1 376.4 %all-reduce.13.cloned.1.call-done = f32[1536,2,1536]{2,1,0:T(2,128)} async-done(((f32[1536,2,1536]{2,1,0:T(2,128)}), f32[1536,2,1536]{2,1,0:T(2,128)}) %all-reduce.13.cloned.1.call-update) | async-done | bytes 18874384
  1488.5 2.6 dynamic-slice_bitcast_fusion.2
  1491.1 3.3 constant_dynamic-slice_fusion.10
  1494.4 1118.8 %all-reduce.15.cloned.1.call-done = f32[1536,2,3072]{2,1,0:T(2,128)} async-done(((f32[1536,2,3072]{2,1,0:T(2,128)}), f32[1536,2,3072]{2,1,0:T(2,128)}) %all-reduce.15.cloned.1.call-update) | async-done | bytes 37748752
  2613.2 7.8 dynamic-slice_bitcast_fusion
  (355 shorter events, 175.8 us)
Async XLA Ops:
  7.2 78.7 %all-reduce.11.cloned.1.call-start = ((), (), s32[]{:S(2)}) async-start(), calls=%async_computation.16 | async-start | bytes 589824
  10.4 3.9 copy-start.65
  10.5 3.9 copy-start.67
  10.5 5.1 copy-start.18
  10.5 5.1 copy-start.19
  10.5 185.5 %all-gather.15.cloned.1.call-start = ((), (), s32[]{:S(2)}) async-start(), calls=%async_computation.5 | async-start | bytes 7962624 | tf_op jit(solution)/shard_map/all_gather | solution.py:120
  14.3 202.7 %all-gather.13.cloned.1.call-start = ((), (), s32[]{:S(2)}) async-start(), calls=%async_computation.4 | async-start | bytes 2181120 | tf_op jit(solution)/shard_map/all_gather | solution.py:95
  24.6 264.2 %copy-start.45 = (s32[2]{0:T(128)}, s32[2]{0:T(128)S(1)}, u32[]{:S(2)}) copy-start(s32[2]{0:T(128)S(1)} %get-tuple-element.240) | copy-start | bytes 28
  24.7 264.2 %copy-start.47 = (s32[2]{0:T(128)}, s32[2]{0:T(128)S(1)}, u32[]{:S(2)}) copy-start(s32[2]{0:T(128)S(1)} %get-tuple-element.315) | copy-start | bytes 28
  24.7 270.1 %copy-start.49 = (s32[2]{0:T(128)}, s32[2]{0:T(128)S(1)}, u32[]{:S(2)}) copy-start(s32[2]{0:T(128)S(1)} %get-tuple-element.241) | copy-start | bytes 28
  24.7 270.1 %copy-start.51 = (s32[2]{0:T(128)}, s32[2]{0:T(128)S(1)}, u32[]{:S(2)}) copy-start(s32[2]{0:T(128)S(1)} %get-tuple-element.314) | copy-start | bytes 28
  24.7 68.8 %copy-start.54 = (f32[564]{0:T(1024)}, f32[564]{0:T(1024)S(1)}, u32[]{:S(2)}) copy-start(f32[564]{0:T(1024)S(1)} %get-tuple-element.312) | copy-start | bytes 6772
  24.7 68.8 %copy-start.56 = (f32[564]{0:T(1024)}, f32[564]{0:T(1024)S(1)}, u32[]{:S(2)}) copy-start(f32[564]{0:T(1024)S(1)} %get-tuple-element.313) | copy-start | bytes 6772
  85.9 7.7 copy-start.44
  88.6 3.1 copy-start.15
  93.6 177.9 %all-gather.23.cloned.1.call-start = ((), (), s32[]{:S(2)}) async-start(), calls=%async_computation.13 | async-start | bytes 2654208 | tf_op jit(solution)/shard_map/all_gather | solution.py:125
  94.4 220.6 %reduce-scatter.6.cloned.1.call-start = ((), (), s32[]{:S(2)}) async-start(), calls=%async_computation.6 | async-start | bytes 4362240 | tf_op jit(solution)/shard_map/reduce_scatter | solution.py:103
  217.0 4.5 copy-start.23
  245.4 28.9 %copy-start.17 = (bf16[6,564,64]{2,1,0:T(8,128)(2,1)}, bf16[6,564,64]{2,1,0:T(8,128)(2,1)S(1)}, u32[]{:S(2)}) copy-start(bf16[6,564,64]{2,1,0:T(8,128)(2,1)S(1)} %get-tuple-element.510) | copy-start | bytes 1299460
  245.4 28.9 %copy-start.28 = (bf16[6,564,64]{2,1,0:T(8,128)(2,1)}, bf16[6,564,64]{2,1,0:T(8,128)(2,1)S(1)}, u32[]{:S(2)}) copy-start(bf16[6,564,64]{2,1,0:T(8,128)(2,1)S(1)} %get-tuple-element.518) | copy-start | bytes 1299460
  276.4 4.2 copy-start.42
  276.4 4.2 copy-start.43
  276.4 5.1 copy-start.40
  276.4 61.2 %all-gather.19.cloned.1.call-start = ((), (), s32[]{:S(2)}) async-start(), calls=%async_computation.9 | async-start | bytes 2181120 | tf_op jit(solution)/shard_map/all_gather | solution.py:99
  281.5 196.2 %all-gather.27.cloned.1.call-start = ((), (), s32[]{:S(2)}) async-start(), calls=%async_computation.15 | async-start | bytes 10616832 | tf_op jit(solution)/shard_map/all_gather | solution.py:125
  282.7 333.2 %all-gather.25.cloned.1.call-start = ((), (), s32[]{:S(2)}) async-start(), calls=%async_computation.14 | async-start | bytes 10616832 | tf_op jit(solution)/shard_map/all_gather | solution.py:120
  285.5 351.3 %all-gather.17.cloned.1.call-start = ((), (), s32[]{:S(2)}) async-start(), calls=%async_computation.7 | async-start | bytes 2181120 | tf_op jit(solution)/shard_map/all_gather | solution.py:95
  288.9 33.8 %copy-start.14 = (f32[256,384]{1,0:T(8,128)}, f32[256,384]{1,0:T(8,128)S(1)}, u32[]{:S(2)}) copy-start(f32[256,384]{1,0:T(8,128)S(1)} %fusion.196) | copy-start | bytes 1179652
  294.8 30.1 %copy-start.7 = (f32[308,384]{1,0:T(8,128)}, f32[308,384]{1,0:T(8,128)S(1)}, u32[]{:S(2)}) copy-start(f32[308,384]{1,0:T(8,128)S(1)} %fusion.163) | copy-start | bytes 1419268
  325.0 369.3 %reduce-scatter.10.cloned.1.call-start = ((), (), s32[]{:S(2)}) async-start(), calls=%async_computation.10 | async-start | bytes 4362240 | tf_op jit(solution)/shard_map/reduce_scatter | solution.py:107
  477.7 5.2 copy-start.33
  636.8 5.4 copy-start.66
  654.2 83.1 %reduce-scatter.8.cloned.1.call-start = ((), (), s32[]{:S(2)}) async-start(), calls=%async_computation.8 | async-start | bytes 4362240 | tf_op jit(solution)/shard_map/reduce_scatter | solution.py:103
  654.3 4.1 copy-start.12
  665.1 99.2 %all-gather.21.cloned.1.call-start = ((), (), s32[]{:S(2)}) async-start(), calls=%async_computation.11 | async-start | bytes 2181120 | tf_op jit(solution)/shard_map/all_gather | solution.py:99
  694.3 43.1 %copy-start.4 = (f32[564,384]{1,0:T(8,128)S(1)}, f32[564,384]{1,0:T(8,128)}, u32[]{:S(2)}) copy-start(f32[564,384]{1,0:T(8,128)} %reduce-scatter.10.cloned.1.call-done) | copy-start | bytes 2598916
  737.4 5.3 copy-start.21
  737.4 5.3 copy-start.24
  743.6 304.8 %reduce-scatter.12.cloned.1.call-start = ((), (), s32[]{:S(2)}) async-start(), calls=%async_computation.12 | async-start | bytes 4362240 | tf_op jit(solution)/shard_map/reduce_scatter | solution.py:107
  759.4 7.3 copy-start.41
  836.3 4.0 copy-start.26
  845.6 642.9 %all-reduce.13.cloned.1.call-start = ((), (), s32[]{:S(2)}) async-start(), calls=%async_computation.17 | async-start | bytes 37748736
  918.3 3.2 copy-start.11
  918.3 1694.9 %all-reduce.15.cloned.1.call-start = ((), (), s32[]{:S(2)}) async-start(), calls=%async_computation.18 | async-start | bytes 75497472
  921.5 5.6 copy-start.13
  921.5 5.6 copy-start.34
  1033.1 7.4 copy-start.5
  1033.1 8.3 copy-start.50
  1033.2 8.3 copy-start.52
  1035.8 15.3 copy-start.9
  1035.8 15.3 copy-start.16
  1035.8 15.4 copy-start.55
  1035.8 15.4 copy-start.57
  1048.3 5.5 copy-start.61
  1048.4 5.5 copy-start.63
  1048.4 5.5 copy-start.62
  1048.4 5.5 copy-start.64
  1048.4 5.5 copy-start.60
  1048.4 5.6 copy-start.59
  1053.1 48.8 %copy-start.3 = (f32[564,384]{1,0:T(8,128)S(1)}, f32[564,384]{1,0:T(8,128)}, u32[]{:S(2)}) copy-start(f32[564,384]{1,0:T(8,128)} %copy-done.2) | copy-start | bytes 2598916
  1053.1 48.8 %copy-start.6 = (f32[564,384]{1,0:T(8,128)S(1)}, f32[564,384]{1,0:T(8,128)}, u32[]{:S(2)}) copy-start(f32[564,384]{1,0:T(8,128)} %reduce-scatter.12.cloned.1.call-done) | copy-start | bytes 2598916
  1101.9 3.4 copy-start.31
  1102.0 3.4 copy-start.53
  1106.9 4.5 copy-start.58
  (19 other events, 35.6 us)
Sparse Core Ops, SparseCore 0:
  11.9 73.9 all-reduce.10
  88.7 107.3 all-gather.14
  198.2 18.7 all-gather.12
  219.6 51.8 all-gather.22
  276.5 38.4 reduce-scatter.5
  317.0 20.5 all-gather.18
  340.4 137.2 all-gather.26
  480.4 135.4 all-gather.24
  618.0 18.7 all-gather.16
  654.3 39.8 reduce-scatter.9
  697.4 39.8 reduce-scatter.7
  743.7 20.5 all-gather.20
  845.7 39.8 reduce-scatter.11
  918.4 570.0 all-reduce.12
  1492.6 1120.5 all-reduce.14
where the time goes:
time: 2640 us; the launch traced here: 2630 us
  waiting for transfers between devices  2070 us (78%)
  local copies, waits for them, and re-layouts  178 us (7%)
  matrix products  171 us (6%)
  other arithmetic  116 us (4%)
  blocking collectives  66.6 us (3%)
    unnamed x18, waiting for transfers between devices  1560 us
    all_gather x2, waiting for transfers between devices, fold_rows(): portion = lax.all_gather(weight, 'row', axis=0, tiled=True)  228 us
    all_gather x2, waiting for transfers between devices, map_rows(): portion = lax.all_gather(weight, 'row', axis=0, tiled=True)  162 us
    another operation x1, local copies, waits for them, and re-layouts, mlp_part(): return jnp.stack([image_part, text_part], axis=1)  55.5 us
  transfers between devices with their start and end apart: 15, of which 14 were waited for; matrix products, arithmetic and copies ran while one was open for 13% of the time, Pallas kernels for 0%

commit v1 on v0

--- a/solution.py
+++ b/solution.py
@@ -11,6 +11,12 @@
 TXT_DEV = 308
 EPSILON = 1e-06
 HIGHEST = lax.Precision.HIGHEST
+
+
+def in_order(blocks, dim):
+    shape = list(blocks.shape[1:])
+    shape[dim] *= blocks.shape[0]
+    return jnp.moveaxis(blocks, 0, dim).reshape(shape)
 
 
 def slot_table(lengths, image_rows, text_rows):
@@ -122,7 +128,19 @@
 
 
 def map_rows(left, weight):
-    portion = lax.all_gather(weight, "row", axis=0, tiled=True)
+    size = lax.axis_size("row")
+    pairs = [(i, (i + 1) % size) for i in range(size)]
+    back = [(b, a) for a, b in pairs]
+    lower_2, upper_2 = ([], [])
+    for step in range(size - 1):
+        if step % 2 == 0:
+            lower_2.append(lax.ppermute(lower_2[-1] if lower_2 else weight, "row", pairs))
+        else:
+            upper_2.append(lax.ppermute(upper_2[-1] if upper_2 else weight, "row", back))
+    pieces = jnp.stack([*lower_2[::-1], weight, *upper_2])
+    shift = lax.axis_index("row") - len(lower_2)
+    pieces = pieces[(jnp.arange(size) - shift) % size]
+    portion = in_order(pieces, 0)
     return stream_dot(left, portion[:, 0].T, portion[:, 1].T)
 
 

time: 2640 us -> 3050 us (1.16)
  local copies, waits for them, and re-layouts: 178 us -> 361 us
  waiting for transfers between devices: 2070 us -> 2220 us
  starting transfers between devices: 10.2 us -> 95.5 us
    ppermute x0 -> x28, waiting for transfers between devices: none -> 495 us  [the longest x16 365 us: map_rows(): lax.ppermute(lower_2[-1] if lower_2 else weight, 'row', pairs)]
    all_gather x2 -> x0, waiting for transfers between devices: 162 us -> none  [map_rows(): portion = lax.all_gather(weight, 'row', axis=0, tiled=True)]
    ppermute x0 -> x28, starting transfers between devices: none -> 94.4 us  [the longest x12 66.2 us: map_rows(): lax.ppermute(upper_2[-1] if upper_2 else weight, 'row', back)]
    gather x0 -> x8, local copies, waits for them, and re-layouts: none -> 93.2 us  [map_rows(): pieces = pieces[(jnp.arange(size) - shift) % size]]
    all_gather x2 -> x4, waiting for transfers between devices: 228 us -> 144 us  [fold_rows(): portion = lax.all_gather(weight, 'row', axis=0, tiled=True)]
    unnamed x142 -> x172, local copies, waits for them, and re-layouts: 17.7 us -> 82.8 us
    reduce_scatter x2, waiting for transfers between devices: 51.9 us -> 0.02 us  [scatter_features(): return lax.psum_scatter(values, 'col', scatter_dimension=1, tiled=True)]
  transfers between devices with their start and end apart: 15 -> 43, of which waited for: 14 -> 23; matrix products, arithmetic and copies ran while one was open for 13% -> 16% of each run, Pallas kernels for 0% -> 0%
where the time goes in v1:
time: 3050 us; the launch traced here: 3040 us
  waiting for transfers between devices  2220 us (73%)
  local copies, waits for them, and re-layouts  361 us (12%)
  matrix products  165 us (5%)
  other arithmetic  117 us (4%)
  starting transfers between devices  95.5 us (3%)
  blocking collectives  64.6 us (2%)
    unnamed x18, waiting for transfers between devices  1560 us
    ppermute x16, waiting for transfers between devices, map_rows(): lax.ppermute(lower_2[-1] if lower_2 else weight, 'row', pairs)  365 us
    all_gather x4, waiting for transfers between devices, fold_rows(): portion = lax.all_gather(weight, 'row', axis=0, tiled=True)  144 us
    ppermute x12, waiting for transfers between devices, map_rows(): lax.ppermute(upper_2[-1] if upper_2 else weight, 'row', back)  130 us
    gather x8, local copies, waits for them, and re-layouts, map_rows(): pieces = pieces[(jnp.arange(size) - shift) % size]  93.2 us
    unnamed x172, local copies, waits for them, and re-layouts  82.8 us
    ppermute x12, starting transfers between devices, map_rows(): lax.ppermute(upper_2[-1] if upper_2 else weight, 'row', back)  66.2 us
  transfers between devices with their start and end apart: 43, of which 23 were waited for; matrix products, arithmetic and copies ran while one was open for 16% of the time, Pallas kernels for 0%

profile of v1, /device:TPU:0, one launch (start us, length us, event | category | flops | bytes accessed | tf_op | source)
XLA Modules:
  0.0 3041.3 jit_solution(1552610614651062959)
XLA Ops:
  22.0 6.8 all-reduce.6
  33.8 62.4 %all-reduce.11.cloned.1.call-done = f32[16,1,2,6,384]{4,0,3,2,1:T(8,128)} async-done(((f32[16,1,2,6,384]{4,0,3,2,1:T(8,128)}), f32[16,1,2,6,384]{4,0,3,2,1:T(8,128)}) %all-reduce.11.cloned.1.call-update) | async-done | bytes 294928
  105.4 12.7 collective-permute-done.2
  126.3 7.5 collective-permute-done.3
  147.8 8.3 gather_fusion
  159.7 52.9 %all-gather.15.cloned.1.call-done = bf16[1536,2,1152]{2,0,1:T(8,128)(2,1)} async-done(((bf16[192,2,1152]{2,0,1:T(8,128)(2,1)}), bf16[1536,2,1152]{2,0,1:T(8,128)(2,1)}) %all-gather.15.cloned.1.call-update) | async-done | bytes 7077904 | tf_op jit(solution)/shard_map/all_gather | solution.py:126
  212.5 6.7 slice_bitcast_fusion.21
  219.2 5.8 copy.135
  225.0 5.8 copy.134
  233.5 4.5 convolution_convert_fusion.4
  245.7 23.8 while.22
  287.5 29.1 collective-permute-done.14
  321.3 59.5 %collective-permute-done.15 = bf16[192,2,1536]{2,1,0:T(2,128)(2,1)} collective-permute-done((bf16[192,2,1536]{2,1,0:T(2,128)(2,1)S(1)}, bf16[192,2,1536]{2,1,0:T(2,128)(2,1)}, u32[]{:S(2)}, u32[]{:S(2)}) %collective-permute-start.15) | collective-permute-done | bytes 1179680 | tf_op jit(solution)/shard_map/ppermute | solution.py:137
  385.6 45.9 %collective-permute-done.7 = bf16[192,2,1536]{2,1,0:T(2,128)(2,1)} collective-permute-done((bf16[192,2,1536]{2,1,0:T(2,128)(2,1)}, bf16[192,2,1536]{2,1,0:T(2,128)(2,1)}, u32[]{:S(2)}, u32[]{:S(2)}) %collective-permute-start.7) | collective-permute-done | bytes 1179680 | tf_op jit(solution)/shard_map/ppermute | solution.py:137
  436.2 69.7 %collective-permute-done.16 = bf16[192,2,1536]{2,1,0:T(2,128)(2,1)} collective-permute-done((bf16[192,2,1536]{2,1,0:T(2,128)(2,1)}, bf16[192,2,1536]{2,1,0:T(2,128)(2,1)}, u32[]{:S(2)}, u32[]{:S(2)}) %collective-permute-start.16) | collective-permute-done | bytes 1179680 | tf_op jit(solution)/shard_map/ppermute | solution.py:137
  519.9 36.6 %collective-permute-done.8 = bf16[192,2,1536]{2,1,0:T(2,128)(2,1)} collective-permute-done((bf16[192,2,1536]{2,1,0:T(2,128)(2,1)}, bf16[192,2,1536]{2,1,0:T(2,128)(2,1)}, u32[]{:S(2)}, u32[]{:S(2)}) %collective-permute-start.8) | collective-permute-done | bytes 1179680 | tf_op jit(solution)/shard_map/ppermute | solution.py:137
  559.0 52.1 %collective-permute-done.19 = bf16[192,2,1536]{2,1,0:T(2,128)(2,1)} collective-permute-done((bf16[192,2,1536]{2,1,0:T(2,128)(2,1)}, bf16[192,2,1536]{2,1,0:T(2,128)(2,1)}, u32[]{:S(2)}, u32[]{:S(2)}) %collective-permute-start.19) | collective-permute-done | bytes 1179680 | tf_op jit(solution)/shard_map/ppermute | solution.py:139
  624.9 6.2 all-reduce.5
  639.5 22.2 collective-permute-done.20
  664.8 24.4 gather_fusion.2
  689.2 9.3 copy.143
  698.5 5.3 fusion.43
  703.8 5.3 fusion.42
  709.0 91.4 %all-gather.23.cloned.1.call-done = bf16[1,1536,2,1536]{3,1,2,0:T(8,128)(2,1)} async-done(((bf16[1,192,2,1536]{3,1,2,0:T(8,128)(2,1)}), bf16[1,1536,2,1536]{3,1,2,0:T(8,128)(2,1)}) %all-gather.23.cloned.1.call-update) | async-done | bytes 9437200 | tf_op jit(solution)/shard_map/all_gather | solution.py:126
  800.4 20.9 all-gather.17.cloned.1.call-done
  821.3 4.4 fusion.46
  825.8 4.1 fusion.47
  829.9 4.1 fusion.64
  839.3 4.3 collective-permute-start.12
  843.6 49.3 %collective-permute-done.12 = bf16[192,2,1536]{2,1,0:T(2,128)(2,1)S(1)} collective-permute-done((bf16[192,2,1536]{2,1,0:T(2,128)(2,1)}, bf16[192,2,1536]{2,1,0:T(2,128)(2,1)S(1)}, u32[]{:S(2)}, u32[]{:S(2)}) %collective-permute-start.12) | collective-permute-done | bytes 1179680 | tf_op jit(solution)/shard_map/ppermute | solution.py:139
  913.7 6.7 collective-permute-done.13
  922.2 24.6 gather_fusion.1
  946.8 9.3 copy.141
  956.1 4.1 fusion.45
  967.6 22.4 collective-permute-done.21
  991.0 4.7 collective-permute-start.25
  995.7 31.5 %collective-permute-done.22 = bf16[192,2,1152]{2,0,1:T(8,128)(2,1)} collective-permute-done((bf16[192,2,1152]{2,0,1:T(8,128)(2,1)S(1)}, bf16[192,2,1152]{2,0,1:T(8,128)(2,1)}, u32[]{:S(2)}, u32[]{:S(2)}) %collective-permute-start.22) | collective-permute-done | bytes 884768 | tf_op jit(solution)/shard_map/ppermute | solution.py:137
  1031.6 14.5 collective-permute-start.26
  1046.1 24.5 collective-permute-done.23
  1076.4 22.6 collective-permute-start.27
  1099.0 23.5 collective-permute-done.24
  1130.7 6.1 all-reduce.4
  1136.9 4.4 convert_multiply_fusion.2
  1153.0 7.3 gather_fusion.3
  1160.4 6.4 copy.154
  1178.6 69.1 %while.23 = (s32[]{:T(128)}, bf16[6,3,564,64]{2,3,0,1:T(8,128)(2,1)}, s32[564]{0:T(1024)S(1)}, bf16[6,564,64]{2,1,0:T(8,128)(2,1)}, bf16[6,564,64]{2,1,0:T(8,128...) while((s32[]{:T(128)}, ...), condition=%wide.region_27.28_spmd, body=%wide.region_25.27_spmd.sunk | while | flops 207346144 | bytes 8020453 | solution.py:320
  1268.7 4.9 fusion.106
  1273.7 8.7 maximum_bitcast_fusion.4
  1282.4 7.9 maximum_bitcast_fusion.3
  1290.3 14.8 pad_maximum_fusion.1
  1305.1 28.4 copy.159
  1336.6 5.0 fusion.114
  1341.6 5.1 fusion.99
  1346.8 5.1 fusion.96
  1351.9 7.8 maximum_bitcast_fusion.2
  1359.7 10.8 maximum_bitcast_fusion.1
  1370.6 21.0 pad_maximum_fusion
  1391.6 55.7 %copy.161 = f32[1536,2,3072]{2,1,0:T(2,128)} copy(f32[1536,2,3072]{0,2,1:T(8,128)} %pad_maximum_fusion) | data formatting | bytes 75497472 | tf_op jit(solution)/shard_map/stack | solution.py:163
  1466.0 33.1 %all-gather.3 = f32[16,2,6,384]{3,1,2,0:T(2,128)S(1)} all-gather(f32[2,2,6,384]{3,1,2,0:T(2,128)S(1)} %copy.155), channel_id=5, replica_groups=mesh['row'=8,'col'=4] {'row'}, dimensions={0}, use_global_device_ids=true | all-gather | bytes 331776 | tf_op jit(solution)/shard_map/all_gather | solution.py:349
  1501.3 12.5 all-reduce.3
  1519.5 4.5 copy.162
  1524.7 377.2 %all-reduce.13.cloned.1.call-done = f32[1536,2,1536]{2,1,0:T(2,128)} async-done(((f32[1536,2,1536]{2,1,0:T(2,128)}), f32[1536,2,1536]{2,1,0:T(2,128)}) %all-reduce.13.cloned.1.call-update) | async-done | bytes 18874384
  1907.7 1118.8 %all-reduce.15.cloned.1.call-done = f32[1536,2,3072]{2,1,0:T(2,128)} async-done(((f32[1536,2,3072]{2,1,0:T(2,128)}), f32[1536,2,3072]{2,1,0:T(2,128)}) %all-reduce.15.cloned.1.call-update) | async-done | bytes 37748752
  3026.6 7.8 dynamic-slice_bitcast_fusion
  (457 shorter events, 364.9 us)
Async XLA Ops:
  7.2 89.0 %all-reduce.11.cloned.1.call-start = ((), (), s32[]{:S(2)}) async-start(), calls=%async_computation.16 | async-start | bytes 589824
  8.7 11.8 copy-start.64
  8.7 11.9 copy-start.65
  8.7 13.0 copy-start.14
  8.7 13.0 copy-start.15
  10.5 202.0 %all-gather.15.cloned.1.call-start = ((), (), s32[]{:S(2)}) async-start(), calls=%async_computation.5 | async-start | bytes 7962624 | tf_op jit(solution)/shard_map/all_gather | solution.py:126
  12.2 111.5 %copy-start.1 = (bf16[1,192,2,3,384]{4,3,1,2,0:T(4,128)(2,1)}, bf16[1,192,2,3,384]{4,3,1,2,0:T(4,128)(2,1)S(1)}, u32[]{:S(2)}) copy-start(bf16[1,192,2,3,384]{4,3,1,2,0:T(4,128)(2,1)S(1)} %copy.133) | copy-start | bytes 2654212
  14.3 219.2 %all-gather.13.cloned.1.call-start = ((), (), s32[]{:S(2)}) async-start(), calls=%async_computation.4 | async-start | bytes 2181120 | tf_op jit(solution)/shard_map/all_gather | solution.py:101
  14.3 17.0 collective-permute-start
  17.4 82.4 %collective-permute-start.4 = (bf16[192,2,384]{2,1,0:T(2,128)(2,1)}, bf16[192,2,384]{2,1,0:T(2,128)(2,1)}, u32[]{:S(2)}, u32[]{:S(2)}) collective-permute-start(bf16[192,2,384]{2,1,0:T(2,128)(2,1)} %bitcast.415), channel_id=1, source_target_pairs={{4,0},{8,4},{12,8},{16,12},{20,16},{24,20},{28,24},{0,28},{5,1},{9... | collective-permute-start | bytes 884744 | tf_op jit(solution)/shard_map/ppermute | solution.py:139
  29.0 482.8 %copy-start.47 = (s32[2]{0:T(128)}, s32[2]{0:T(128)S(1)}, u32[]{:S(2)}) copy-start(s32[2]{0:T(128)S(1)} %get-tuple-element.240) | copy-start | bytes 28
  29.0 482.8 %copy-start.49 = (s32[2]{0:T(128)}, s32[2]{0:T(128)S(1)}, u32[]{:S(2)}) copy-start(s32[2]{0:T(128)S(1)} %get-tuple-element.315) | copy-start | bytes 28
  29.0 488.6 %copy-start.51 = (s32[2]{0:T(128)}, s32[2]{0:T(128)S(1)}, u32[]{:S(2)}) copy-start(s32[2]{0:T(128)S(1)} %get-tuple-element.241) | copy-start | bytes 28
  29.0 488.6 %copy-start.53 = (s32[2]{0:T(128)}, s32[2]{0:T(128)S(1)}, u32[]{:S(2)}) copy-start(s32[2]{0:T(128)S(1)} %get-tuple-element.314) | copy-start | bytes 28
  29.3 112.0 %copy-start.56 = (f32[564]{0:T(1024)}, f32[564]{0:T(1024)S(1)}, u32[]{:S(2)}) copy-start(f32[564]{0:T(1024)S(1)} %get-tuple-element.312) | copy-start | bytes 6772
  29.3 112.0 %copy-start.58 = (f32[564]{0:T(1024)}, f32[564]{0:T(1024)S(1)}, u32[]{:S(2)}) copy-start(f32[564]{0:T(1024)S(1)} %get-tuple-element.313) | copy-start | bytes 6772
  31.3 66.4 %collective-permute-start.1 = (bf16[192,2,384]{2,1,0:T(2,128)(2,1)}, bf16[192,2,384]{2,1,0:T(2,128)(2,1)}, u32[]{:S(2)}, u32[]{:S(2)}) collective-permute-start(bf16[192,2,384]{2,1,0:T(2,128)(2,1)} %collective-permute-done), channel_id=1, source_target_pairs={{0,4},{4,8},{8,12},{12,16},{16,20},{20,24},{24,28},{28,0},{1,5},{5... | collective-permute-start | bytes 884744 | tf_op jit(solution)/shard_map/ppermute | solution.py:137
  97.7 20.3 collective-permute-start.2
  99.8 23.9 collective-permute-start.5
  105.4 16.5 copy-start.8
  118.0 15.7 collective-permute-start.3
  123.7 499.4 %reduce-scatter.6.cloned.1.call-start = ((), (), s32[]{:S(2)}) async-start(), calls=%async_computation.6 | async-start | bytes 4362240 | tf_op jit(solution)/shard_map/reduce_scatter | solution.py:109
  123.7 23.2 collective-permute-start.6
  276.8 421.7 %all-gather.19.cloned.1.call-start = ((), (), s32[]{:S(2)}) async-start(), calls=%async_computation.9 | async-start | bytes 2181120 | tf_op jit(solution)/shard_map/all_gather | solution.py:105
  281.9 416.6 %all-gather.25.cloned.1.call-start = ((), (), s32[]{:S(2)}) async-start(), calls=%async_computation.14 | async-start | bytes 10616832 | tf_op jit(solution)/shard_map/all_gather | solution.py:126
  284.4 516.0 %all-gather.23.cloned.1.call-start = ((), (), s32[]{:S(2)}) async-start(), calls=%async_computation.13 | async-start | bytes 10616832 | tf_op jit(solution)/shard_map/all_gather | solution.py:126
  285.7 535.7 %all-gather.17.cloned.1.call-start = ((), (), s32[]{:S(2)}) async-start(), calls=%async_computation.7 | async-start | bytes 2181120 | tf_op jit(solution)/shard_map/all_gather | solution.py:101
  285.7 30.8 %collective-permute-start.14 = (bf16[192,2,1536]{2,1,0:T(2,128)(2,1)S(1)}, bf16[192,2,1536]{2,1,0:T(2,128)(2,1)S(1)}, u32[]{:S(2)}, u32[]{:S(2)}) collective-permute-start(bf16[192,2,1536]{2,1,0:T(2,128)(2,1)S(1)} %bitcast.392), channel_id=1, source_target_pairs={{0,4},{4,8},{8,12},{12,16},{16,20},{20,24},{24,28},{28,0},{1,5},{5... | collective-permute-start | bytes 3538952 | tf_op jit(solution)/shard_map/ppermute | solution.py:137
  316.6 64.3 %collective-permute-start.15 = (bf16[192,2,1536]{2,1,0:T(2,128)(2,1)S(1)}, bf16[192,2,1536]{2,1,0:T(2,128)(2,1)}, u32[]{:S(2)}, u32[]{:S(2)}) collective-permute-start(bf16[192,2,1536]{2,1,0:T(2,128)(2,1)S(1)} %collective-permute-done.14), channel_id=1, source_target_pairs={{0,4},{4,8},{8,12},{12,16},{16,20},{20,24},{24,28},{28,0},{1,5},{5... | collective-permute-start | bytes 3538952 | tf_op jit(solution)/shard_map/ppermute | solution.py:137
  316.6 114.9 %collective-permute-start.7 = (bf16[192,2,1536]{2,1,0:T(2,128)(2,1)}, bf16[192,2,1536]{2,1,0:T(2,128)(2,1)}, u32[]{:S(2)}, u32[]{:S(2)}) collective-permute-start(bf16[192,2,1536]{2,1,0:T(2,128)(2,1)} %bitcast.394), channel_id=1, source_target_pairs={{0,4},{4,8},{8,12},{12,16},{16,20},{20,24},{24,28},{28,0},{1,5},{5... | collective-permute-start | bytes 3538952 | tf_op jit(solution)/shard_map/ppermute | solution.py:137
  317.9 116.1 %collective-permute-start.18 = (bf16[192,2,1536]{2,1,0:T(2,128)(2,1)S(1)}, bf16[192,2,1536]{2,1,0:T(2,128)(2,1)}, u32[]{:S(2)}, u32[]{:S(2)}) collective-permute-start(bf16[192,2,1536]{2,1,0:T(2,128)(2,1)S(1)} %bitcast.393), channel_id=1, source_target_pairs={{4,0},{8,4},{12,8},{16,12},{20,16},{24,20},{28,24},{0,28},{5,1},{9... | collective-permute-start | bytes 3538952 | tf_op jit(solution)/shard_map/ppermute | solution.py:139
  380.8 125.1 %collective-permute-start.16 = (bf16[192,2,1536]{2,1,0:T(2,128)(2,1)}, bf16[192,2,1536]{2,1,0:T(2,128)(2,1)}, u32[]{:S(2)}, u32[]{:S(2)}) collective-permute-start(bf16[192,2,1536]{2,1,0:T(2,128)(2,1)} %collective-permute-done.15), channel_id=1, source_target_pairs={{0,4},{4,8},{8,12},{12,16},{16,20},{20,24},{24,28},{28,0},{1,5},{5... | collective-permute-start | bytes 3538952 | tf_op jit(solution)/shard_map/ppermute | solution.py:137
  383.4 455.9 %collective-permute-start.11 = (bf16[192,2,1536]{2,1,0:T(2,128)(2,1)}, bf16[192,2,1536]{2,1,0:T(2,128)(2,1)}, u32[]{:S(2)}, u32[]{:S(2)}) collective-permute-start(bf16[192,2,1536]{2,1,0:T(2,128)(2,1)} %bitcast.395), channel_id=1, source_target_pairs={{4,0},{8,4},{12,8},{16,12},{20,16},{24,20},{28,24},{0,28},{5,1},{9... | collective-permute-start | bytes 3538952 | tf_op jit(solution)/shard_map/ppermute | solution.py:139
  431.5 125.0 %collective-permute-start.8 = (bf16[192,2,1536]{2,1,0:T(2,128)(2,1)}, bf16[192,2,1536]{2,1,0:T(2,128)(2,1)}, u32[]{:S(2)}, u32[]{:S(2)}) collective-permute-start(bf16[192,2,1536]{2,1,0:T(2,128)(2,1)} %collective-permute-done.7), channel_id=1, source_target_pairs={{0,4},{4,8},{8,12},{12,16},{16,20},{20,24},{24,28},{28,0},{1,5},{5... | collective-permute-start | bytes 3538952 | tf_op jit(solution)/shard_map/ppermute | solution.py:137
  434.0 177.1 %collective-permute-start.19 = (bf16[192,2,1536]{2,1,0:T(2,128)(2,1)}, bf16[192,2,1536]{2,1,0:T(2,128)(2,1)}, u32[]{:S(2)}, u32[]{:S(2)}) collective-permute-start(bf16[192,2,1536]{2,1,0:T(2,128)(2,1)} %collective-permute-done.18), channel_id=1, source_target_pairs={{4,0},{8,4},{12,8},{16,12},{20,16},{24,20},{28,24},{0,28},{5,1},{9... | collective-permute-start | bytes 3538952 | tf_op jit(solution)/shard_map/ppermute | solution.py:139
  505.9 105.2 %collective-permute-start.17 = (bf16[192,2,1536]{2,1,0:T(2,128)(2,1)}, bf16[192,2,1536]{2,1,0:T(2,128)(2,1)S(1)}, u32[]{:S(2)}, u32[]{:S(2)}) collective-permute-start(bf16[192,2,1536]{2,1,0:T(2,128)(2,1)} %collective-permute-done.16), channel_id=1, source_target_pairs={{0,4},{4,8},{8,12},{12,16},{16,20},{20,24},{24,28},{28,0},{1,5},{5... | collective-permute-start | bytes 3538952 | tf_op jit(solution)/shard_map/ppermute | solution.py:137
  519.9 99.5 %copy-start.42 = (bf16[192,2,1536]{2,1,0:T(2,128)(2,1)S(1)}, bf16[192,2,1536]{2,1,0:T(2,128)(2,1)}, u32[]{:S(2)}) copy-start(bf16[192,2,1536]{2,1,0:T(2,128)(2,1)} %copy-done.41) | copy-start | bytes 3538948
  556.5 287.1 %collective-permute-start.9 = (bf16[192,2,1536]{2,1,0:T(2,128)(2,1)}, bf16[192,2,1536]{2,1,0:T(2,128)(2,1)}, u32[]{:S(2)}, u32[]{:S(2)}) collective-permute-start(bf16[192,2,1536]{2,1,0:T(2,128)(2,1)} %collective-permute-done.8), channel_id=1, source_target_pairs={{0,4},{4,8},{8,12},{12,16},{16,20},{20,24},{24,28},{28,0},{1,5},{5... | collective-permute-start | bytes 3538952 | tf_op jit(solution)/shard_map/ppermute | solution.py:137
  611.1 50.6 %collective-permute-start.20 = (bf16[192,2,1536]{2,1,0:T(2,128)(2,1)}, bf16[192,2,1536]{2,1,0:T(2,128)(2,1)}, u32[]{:S(2)}, u32[]{:S(2)}) collective-permute-start(bf16[192,2,1536]{2,1,0:T(2,128)(2,1)} %collective-permute-done.19), channel_id=1, source_target_pairs={{4,0},{8,4},{12,8},{16,12},{20,16},{24,20},{28,24},{0,28},{5,1},{9... | collective-permute-start | bytes 3538952 | tf_op jit(solution)/shard_map/ppermute | solution.py:139
  633.3 495.8 %reduce-scatter.10.cloned.1.call-start = ((), (), s32[]{:S(2)}) async-start(), calls=%async_computation.10 | async-start | bytes 4362240 | tf_op jit(solution)/shard_map/reduce_scatter | solution.py:113
  839.2 297.6 %reduce-scatter.8.cloned.1.call-start = ((), (), s32[]{:S(2)}) async-start(), calls=%async_computation.8 | async-start | bytes 4362240 | tf_op jit(solution)/shard_map/reduce_scatter | solution.py:109
  839.3 53.6 %collective-permute-start.12 = (bf16[192,2,1536]{2,1,0:T(2,128)(2,1)}, bf16[192,2,1536]{2,1,0:T(2,128)(2,1)S(1)}, u32[]{:S(2)}, u32[]{:S(2)}) collective-permute-start(bf16[192,2,1536]{2,1,0:T(2,128)(2,1)} %collective-permute-done.11), channel_id=1, source_target_pairs={{4,0},{8,4},{12,8},{16,12},{20,16},{24,20},{28,24},{0,28},{5,1},{9... | collective-permute-start | bytes 3538952 | tf_op jit(solution)/shard_map/ppermute | solution.py:139
  843.6 52.0 %collective-permute-start.10 = (bf16[192,2,1536]{2,1,0:T(2,128)(2,1)}, bf16[192,2,1536]{2,1,0:T(2,128)(2,1)S(1)}, u32[]{:S(2)}, u32[]{:S(2)}) collective-permute-start(bf16[192,2,1536]{2,1,0:T(2,128)(2,1)} %collective-permute-done.9), channel_id=1, source_target_pairs={{0,4},{4,8},{8,12},{12,16},{16,20},{20,24},{24,28},{28,0},{1,5},{5... | collective-permute-start | bytes 3538952 | tf_op jit(solution)/shard_map/ppermute | solution.py:137
  892.9 27.4 collective-permute-start.13
  897.4 9.4 copy-start.18
  966.3 200.5 %all-gather.27.cloned.1.call-start = ((), (), s32[]{:S(2)}) async-start(), calls=%async_computation.15 | async-start | bytes 2654208 | tf_op jit(solution)/shard_map/all_gather | solution.py:126
  966.4 23.7 collective-permute-start.21
  991.0 36.2 %collective-permute-start.22 = (bf16[192,2,1152]{2,0,1:T(8,128)(2,1)S(1)}, bf16[192,2,1152]{2,0,1:T(8,128)(2,1)}, u32[]{:S(2)}, u32[]{:S(2)}) collective-permute-start(bf16[192,2,1152]{2,0,1:T(8,128)(2,1)S(1)} %collective-permute-done.21), channel_id=1, source_target_pairs={{0,4},{4,8},{8,12},{12,16},{16,20},{20,24},{24,28},{28,0},{1,5},{5... | collective-permute-start | bytes 2654216 | tf_op jit(solution)/shard_map/ppermute | solution.py:137
  991.0 40.6 %collective-permute-start.25 = (bf16[192,2,1152]{2,0,1:T(8,128)(2,1)}, bf16[192,2,1152]{2,0,1:T(8,128)(2,1)}, u32[]{:S(2)}, u32[]{:S(2)}) collective-permute-start(bf16[192,2,1152]{2,0,1:T(8,128)(2,1)} %reshape_squeeze.4), channel_id=1, source_target_pairs={{4,0},{8,4},{12,8},{16,12},{20,16},{24,20},{28,24},{0,28},{5,1},{9... | collective-permute-start | bytes 2654216 | tf_op jit(solution)/shard_map/ppermute | solution.py:139
  1027.3 43.4 %collective-permute-start.23 = (bf16[192,2,1152]{2,0,1:T(8,128)(2,1)}, bf16[192,2,1152]{2,0,1:T(8,128)(2,1)}, u32[]{:S(2)}, u32[]{:S(2)}) collective-permute-start(bf16[192,2,1152]{2,0,1:T(8,128)(2,1)} %collective-permute-done.22), channel_id=1, source_target_pairs={{0,4},{4,8},{8,12},{12,16},{16,20},{20,24},{24,28},{28,0},{1,5},{5... | collective-permute-start | bytes 2654216 | tf_op jit(solution)/shard_map/ppermute | solution.py:137
  1031.6 142.1 %all-gather.21.cloned.1.call-start = ((), (), s32[]{:S(2)}) async-start(), calls=%async_computation.11 | async-start | bytes 2181120 | tf_op jit(solution)/shard_map/all_gather | solution.py:105
  1031.6 44.8 %collective-permute-start.26 = (bf16[192,2,1152]{2,0,1:T(8,128)(2,1)}, bf16[192,2,1152]{2,0,1:T(8,128)(2,1)}, u32[]{:S(2)}, u32[]{:S(2)}) collective-permute-start(bf16[192,2,1152]{2,0,1:T(8,128)(2,1)} %collective-permute-done.25), channel_id=1, source_target_pairs={{4,0},{8,4},{12,8},{16,12},{20,16},{24,20},{28,24},{0,28},{5,1},{9... | collective-permute-start | bytes 2654216 | tf_op jit(solution)/shard_map/ppermute | solution.py:139
  1070.6 51.9 %collective-permute-start.24 = (bf16[192,2,1152]{2,0,1:T(8,128)(2,1)}, bf16[192,2,1152]{2,0,1:T(8,128)(2,1)}, u32[]{:S(2)}, u32[]{:S(2)}) collective-permute-start(bf16[192,2,1152]{2,0,1:T(8,128)(2,1)} %collective-permute-done.23), channel_id=1, source_target_pairs={{0,4},{4,8},{8,12},{12,16},{16,20},{20,24},{24,28},{28,0},{1,5},{5... | collective-permute-start | bytes 2654216 | tf_op jit(solution)/shard_map/ppermute | solution.py:137
  1076.4 74.4 %collective-permute-start.27 = (bf16[192,2,1152]{2,0,1:T(8,128)(2,1)}, bf16[192,2,1152]{2,0,1:T(8,128)(2,1)}, u32[]{:S(2)}, u32[]{:S(2)}) collective-permute-start(bf16[192,2,1152]{2,0,1:T(8,128)(2,1)} %collective-permute-done.26), channel_id=1, source_target_pairs={{4,0},{8,4},{12,8},{16,12},{20,16},{24,20},{28,24},{0,28},{5,1},{9... | collective-permute-start | bytes 2654216 | tf_op jit(solution)/shard_map/ppermute | solution.py:139
  1143.1 315.8 %reduce-scatter.12.cloned.1.call-start = ((), (), s32[]{:S(2)}) async-start(), calls=%async_computation.12 | async-start | bytes 4362240 | tf_op jit(solution)/shard_map/reduce_scatter | solution.py:113
  1259.4 642.4 %all-reduce.13.cloned.1.call-start = ((), (), s32[]{:S(2)}) async-start(), calls=%async_computation.17 | async-start | bytes 37748736
  1333.6 1693.0 %all-reduce.15.cloned.1.call-start = ((), (), s32[]{:S(2)}) async-start(), calls=%async_computation.18 | async-start | bytes 75497472
  1447.3 9.0 copy-start.52
  1447.3 14.6 copy-start.57
  1447.3 14.6 copy-start.59
  1448.0 9.2 copy-start.26
  1460.3 54.3 %copy-start.5 = (f32[564,384]{1,0:T(8,128)S(1)}, f32[564,384]{1,0:T(8,128)}, u32[]{:S(2)}) copy-start(f32[564,384]{1,0:T(8,128)} %copy-done.4) | copy-start | bytes 2598916
  1460.3 54.2 %copy-start.7 = (f32[564,384]{1,0:T(8,128)S(1)}, f32[564,384]{1,0:T(8,128)}, u32[]{:S(2)}) copy-start(f32[564,384]{1,0:T(8,128)} %reduce-scatter.12.cloned.1.call-done) | copy-start | bytes 2598916
  1499.9 18.0 copy-start.55
  (48 other events, 230.3 us)
Sparse Core Ops, SparseCore 0:
  11.9 84.2 all-reduce.10
  98.4 114.1 all-gather.14
  214.7 18.7 all-gather.12
  276.9 39.8 reduce-scatter.5
  318.2 20.5 all-gather.18
  341.4 320.2 all-gather.24
  664.6 135.7 all-gather.22
  802.5 18.7 all-gather.16
  839.3 39.8 reduce-scatter.9
  966.5 40.7 reduce-scatter.7
  1031.7 94.6 all-gather.26
  1143.2 18.8 all-gather.20
  1259.6 37.9 reduce-scatter.11
  1333.7 568.1 all-reduce.12
  1906.0 1120.5 all-reduce.14
